TPU v7x, 32 devices: a whole 2x2x4 slice. The times are simulated.
32 devices in a mesh: batch: 4 (over y, core), tensor: 2 (over x), latent: 4 (over z).
Axes of the slice: x: 2, y: 2, z: 4, core: 2. Of those that a mesh axis runs over, the one named last changes fastest.
Arguments:
- residual: bfloat16 [1024, 3584], P('batch', ('tensor', 'latent')), may hold values from -6 to 6
- target: bfloat16 [1024, 3584], P('batch', ('tensor', 'latent')), may hold values from -6 to 6
- encoder_weight: bfloat16 [3584, 32768], P(None, ('tensor', 'latent')), may hold values from -0.09375 to 0.09375
- encoder_bias: bfloat16 [32768], P(('tensor', 'latent')), may hold values from -0.59765625 to 0.29882812
- decoder_weight: bfloat16 [32768, 3584], P(('tensor', 'latent')), may hold values from -0.0625 to 0.0625
- decoder_bias: bfloat16 [3584], replicated, may hold values from -3 to 3
- first_gain: bfloat16 [3584], replicated, may hold values from 0.5 to 1.5
- second_gain: bfloat16 [3584], replicated, may hold values from 0.5 to 1.5
- gate_weight: bfloat16 [3584, 7168], P(None, ('tensor', 'latent')), may hold values from -0.09375 to 0.09375
- up_weight: bfloat16 [3584, 7168], P(None, ('tensor', 'latent')), may hold values from -0.09375 to 0.09375
- down_weight: bfloat16 [7168, 3584], P(('tensor', 'latent')), may hold values from -0.09375 to 0.09375
Outputs:
- encoder_grad: bfloat16 [3584, 32768], P('batch', ('tensor', 'latent'))
- decoder_grad: bfloat16 [32768, 3584], P(('tensor', 'latent'), 'batch')
All inputs are finite; a program needn't handle non-finite values.
Results may differ from a plain program's by a relative error of at most 0.012.
The roundings to bfloat16 on the way count: a program that leaves them out, or rounds other values in their place, can miss the bound.
Values may be sent and summed in bfloat16 or wider, within the bound.
A program may use at most 192 MiB of HBM per device.

v0:
```python
import jax
import jax.numpy as jnp
from jax import lax
from jax.sharding import PartitionSpec as P

epsilon = 1e-06


def per_device(
    residual,
    target,
    encoder_weight,
    encoder_bias,
    decoder_weight,
    decoder_bias,
    first_gain,
    second_gain,
    gate_weight,
    up_weight,
    down_weight,
):
    f32 = jnp.float32
    bf16 = jnp.bfloat16
    contract_last = (((1,), (1,)), ((), ()))
    contract_first = (((0,), (0,)), ((), ()))
    share_width = residual.shape[1]
    model_width = share_width * lax.axis_size(("tensor", "latent"))
    offset = lax.axis_index(("tensor", "latent")) * share_width
    token_count = residual.shape[0] * lax.axis_size("batch")
    bias_share = lax.dynamic_slice_in_dim(decoder_bias.astype(f32), offset, share_width)
    first_share = lax.dynamic_slice_in_dim(first_gain.astype(f32), offset, share_width)
    second_share = lax.dynamic_slice_in_dim(second_gain.astype(f32), offset, share_width)
    centered_share = (residual.astype(f32) - bias_share).astype(bf16)
    centered = lax.all_gather(centered_share, ("tensor", "latent"), axis=1, tiled=True)
    preact = jnp.dot(centered, encoder_weight, preferred_element_type=f32) + encoder_bias.astype(
        f32
    )
    latents = jnp.maximum(preact, 0.0).astype(bf16)
    partial_recon = jnp.dot(latents, decoder_weight, preferred_element_type=f32)
    recon_full = lax.psum(partial_recon.astype(jnp.bfloat16), ("tensor", "latent")).astype(
        jnp.float32
    ) + decoder_bias.astype(f32)
    scale_in = lax.rsqrt(
        jnp.sum(recon_full * recon_full, axis=1, keepdims=True) / model_width + epsilon
    )
    normed_input = (recon_full * scale_in * first_gain.astype(f32)).astype(bf16)
    recon = lax.dynamic_slice_in_dim(recon_full, offset, share_width, 1)
    gate_value = jnp.dot(normed_input, gate_weight, preferred_element_type=f32)
    up_value = jnp.dot(normed_input, up_weight, preferred_element_type=f32)
    gelu_value, gelu_back = jax.vjp(lambda v: jax.nn.gelu(v, approximate=True), gate_value)
    hidden = (gelu_value * up_value).astype(bf16)
    partial_out = jnp.dot(hidden, down_weight, preferred_element_type=f32)
    output = lax.psum_scatter(
        partial_out.astype(jnp.bfloat16), ("tensor", "latent"), scatter_dimension=1, tiled=True
    ).astype(jnp.float32)
    out_squares = lax.psum(jnp.sum(output * output, axis=1), ("tensor", "latent"))
    scale_out = lax.rsqrt(out_squares[:, None] / model_width + epsilon)
    normed_out = output * scale_out
    result = recon + normed_out * second_share
    grad_result = 2.0 * (result - target.astype(f32)) / token_count
    grad_normed = grad_result * second_share
    inner_out = (
        lax.psum(jnp.sum(grad_normed * normed_out, axis=1), ("tensor", "latent")) / model_width
    )
    grad_share = (scale_out * (grad_normed - normed_out * inner_out[:, None])).astype(bf16)
    grad_output = lax.all_gather(grad_share, ("tensor", "latent"), axis=1, tiled=True)
    grad_hidden = lax.dot_general(
        grad_output, down_weight, contract_last, preferred_element_type=f32
    )
    grad_gate = gelu_back(grad_hidden * up_value)[0].astype(bf16)
    grad_up = (grad_hidden * gelu_value).astype(bf16)
    partial_input = lax.dot_general(
        grad_gate, gate_weight, contract_last, preferred_element_type=f32
    )
    partial_input = partial_input + lax.dot_general(
        grad_up, up_weight, contract_last, preferred_element_type=f32
    )
    grad_normed_in = lax.psum_scatter(
        partial_input.astype(jnp.bfloat16), ("tensor", "latent"), scatter_dimension=1, tiled=True
    ).astype(jnp.float32)
    unit = recon * scale_in
    grad_unit = grad_normed_in * first_share
    inner_in = lax.psum(jnp.sum(grad_unit * unit, axis=1), ("tensor", "latent")) / model_width
    recon_share = (grad_result + scale_in * (grad_unit - unit * inner_in[:, None])).astype(bf16)
    grad_recon = lax.all_gather(recon_share, ("tensor", "latent"), axis=1, tiled=True)
    grad_latent = lax.dot_general(
        grad_recon, decoder_weight, contract_last, preferred_element_type=f32
    )
    grad_preact = jnp.where(preact > 0, grad_latent, 0.0).astype(bf16)
    centered_block, recon_block = (
        lax.all_to_all(centered, "batch", split_axis=1, concat_axis=0, tiled=True),
        lax.all_to_all(grad_recon, "batch", split_axis=1, concat_axis=0, tiled=True),
    )
    latents_all, preact_all = (
        lax.all_gather(latents, "batch", axis=0, tiled=True),
        lax.all_gather(grad_preact, "batch", axis=0, tiled=True),
    )
    encoder_grad = lax.dot_general(
        centered_block, preact_all, contract_first, preferred_element_type=f32
    )
    decoder_grad = lax.dot_general(
        latents_all, recon_block, contract_first, preferred_element_type=f32
    )
    return (encoder_grad.astype(bf16), decoder_grad.astype(bf16))


def solution(mesh):
    in_specs = (
        P("batch", ("tensor", "latent")),
        P("batch", ("tensor", "latent")),
        P(None, ("tensor", "latent")),
        P(("tensor", "latent")),
        P(("tensor", "latent"), None),
        P(),
        P(),
        P(),
        P(None, ("tensor", "latent")),
        P(None, ("tensor", "latent")),
        P(("tensor", "latent"), None),
    )
    out_specs = (P("batch", ("tensor", "latent")), P(("tensor", "latent"), "batch"))
    return jax.shard_map(
        per_device, mesh=mesh, in_specs=in_specs, out_specs=out_specs, check_vma=False
    )
```

profile of v0, /device:TPU:0, one launch (start us, length us, event | category | flops | bytes accessed | tf_op | source)
XLA Modules:
  0.0 670.3 jit_solution(1007464066563289429)
XLA Ops:
  10.5 49.3 %all-gather.6.cloned.1.call-done = bf16[256,3584]{0,1:T(8,128)(2,1)} async-done(((bf16[256,448]{0,1:T(8,128)(2,1)}), bf16[256,3584]{0,1:T(8,128)(2,1)}) %all-gather.6.cloned.1.call-update) | async-done | bytes 1835024 | tf_op jit(solution)/shard_map/all_gather | solution.py:34
  59.8 15.2 %maximum_convert_fusion = (bf16[256,4096]{1,0:T(8,128)(2,1)S(1)}, f32[256,4096]{1,0:T(8,128)}) fusion(f32[4096]{0:T(1024)S(1)} %convert_element_type.74, bf16[256,3584]{0,1:T(8,128)(2,1)} %all-gather.6.cloned.1.call-done, bf16[3584,4096]{1,0:T(8,128)(2,1)} %param.13), kind=kOutput, calls=%fused_computation.11 | convolution fusion | flops 7519338496 | bytes 37502976 | tf_op jit(solution)/shard_map/dot_general | solution.py:35
  75.0 15.5 %convolution_convert_fusion.2 = bf16[256,3584]{1,0:T(8,128)(2,1)} fusion(bf16[256,4096]{1,0:T(8,128)(2,1)S(1)} %get-tuple-element.4, bf16[4096,3584]{1,0:T(8,128)(2,1)} %param.15), kind=kOutput, calls=%fused_computation.5 | convolution fusion | flops 7517110272 | bytes 33292288 | tf_op jit(solution)/shard_map/dot_general | solution.py:39
  90.7 94.5 %all-reduce.2.cloned.1.call-done = bf16[256,3584]{1,0:T(8,128)(2,1)} async-done(((bf16[256,3584]{1,0:T(8,128)(2,1)}), bf16[256,3584]{1,0:T(8,128)(2,1)}) %all-reduce.2.cloned.1.call-update) | async-done | bytes 1835024 | tf_op jit(solution)/shard_map/psum | solution.py:40
  185.2 4.0 convert_add_fusion
  189.2 5.6 fusion.30
  197.1 4.3 fusion.2
  203.1 64.5 %reduce-scatter.7.cloned.1.call-done = bf16[448,256]{1,0:T(8,128)(2,1)} async-done(((bf16[3584,256]{1,0:T(8,128)(2,1)}), bf16[448,256]{1,0:T(8,128)(2,1)}) %reduce-scatter.7.cloned.1.call-update) | async-done | bytes 229392
  268.9 19.4 %psum.29 = f32[256]{0:T(256)S(1)} all-reduce(f32[256]{0:T(256)S(1)} %fusion.20), channel_id=1, replica_groups=mesh['batch'=4,'tensor'=2,'latent'=4] {'tensor','latent'}, use_global_device_ids=true, to_apply=%region_4.0 | all-reduce | flops 256 | bytes 2048 | tf_op jit(solution)/shard_map/psum | solution.py:56
  289.7 17.2 %psum.30 = f32[256]{0:T(256)S(1)} all-reduce(f32[256]{0:T(256)S(1)} %fusion.16), channel_id=1, replica_groups=mesh['batch'=4,'tensor'=2,'latent'=4] {'tensor','latent'}, use_global_device_ids=true, to_apply=%region_6.0 | all-reduce | flops 256 | bytes 2048 | tf_op jit(solution)/shard_map/psum | solution.py:63
  309.5 45.8 %all-gather.8.cloned.1.call-done = bf16[256,3584]{0,1:T(8,128)(2,1)} async-done(((bf16[256,448]{0,1:T(8,128)(2,1)}), bf16[256,3584]{0,1:T(8,128)(2,1)}) %all-gather.8.cloned.1.call-update) | async-done | bytes 1835024 | tf_op jit(solution)/shard_map/all_gather | solution.py:66
  355.3 5.6 fusion.45
  361.0 5.4 fusion.21
  366.5 3.6 fusion.3
  370.3 65.2 %reduce-scatter.9.cloned.1.call-done = bf16[448,256]{1,0:T(8,128)(2,1)} async-done(((bf16[3584,256]{1,0:T(8,128)(2,1)}), bf16[448,256]{1,0:T(8,128)(2,1)}) %reduce-scatter.9.cloned.1.call-update) | async-done | bytes 229392
  438.0 19.3 %psum.31 = f32[256]{0:T(256)S(1)} all-reduce(f32[256]{0:T(256)S(1)} %multiply_reduce_fusion.1), channel_id=1, replica_groups=mesh['batch'=4,'tensor'=2,'latent'=4] {'tensor','latent'}, use_global_device_ids=true, to_apply=%region_9.0 | all-reduce | flops 256 | bytes 2048 | tf_op jit(solution)/shard_map/psum | solution.py:83
  460.5 44.0 %all-gather.10.cloned.1.call-done = bf16[256,3584]{0,1:T(8,128)(2,1)} async-done(((bf16[256,448]{0,1:T(8,128)(2,1)}), bf16[256,3584]{0,1:T(8,128)(2,1)}) %all-gather.10.cloned.1.call-update) | async-done | bytes 1835024 | tf_op jit(solution)/shard_map/all_gather | solution.py:85
  504.5 18.3 %fusion = bf16[256,4096]{1,0:T(8,128)(2,1)} fusion(bf16[256,3584]{0,1:T(8,128)(2,1)} %all-gather.10.cloned.1.call-done, bf16[4096,3584]{1,0:T(8,128)(2,1)} %param.15, f32[256,4096]{1,0:T(8,128)} %get-tuple-element.5), kind=kOutput, calls=%fused_computation.6 | convolution fusion | flops 7519338496 | bytes 37486592 | tf_op jit(solution)/shard_map/dot_general | solution.py:86
  522.8 46.2 %all_to_all.38 = bf16[256,4,896]{0,2,1:T(8,128)(2,1)} all-to-all(bf16[256,4,896]{0,2,1:T(8,128)(2,1)S(1)} %bitcast.35), channel_id=1, replica_groups=mesh['batch'=4,'tensor'=2,'latent'=4] {'batch'}, dimensions={1} | all-to-all | bytes 3670016 | tf_op jit(solution)/shard_map/all_to_all | solution.py:91
  569.0 3.8 all-to-all-start.1
  576.5 24.1 %all-to-all-done.1 = bf16[256,4,896]{0,2,1:T(8,128)(2,1)S(1)} async-done(((bf16[256,4,896]{0,2,1:T(8,128)(2,1)}), bf16[256,4,896]{0,2,1:T(8,128)(2,1)S(1)}, u32[]{:S(2)}, u32[]{:S(2)}) %all-to-all-start.1) | async-done | bytes 1835040 | tf_op jit(solution)/shard_map/all_to_all | solution.py:92
  603.0 15.2 %convolution_convert_fusion = bf16[4096,896]{1,0:T(8,128)(2,1)} fusion(bf16[1024,4096]{1,0:T(8,128)(2,1)} %all-gather.14.cloned.1.call-done, bf16[1024,896]{1,0:T(8,128)(2,1)} %bitcast.38), kind=kOutput, calls=%fused_computation | convolution fusion | flops 7519862784 | bytes 17563648 | tf_op jit(solution)/shard_map/dot_general | solution.py:101
  618.1 33.3 %all-gather.12.cloned.1.call-done = bf16[1024,4096]{1,0:T(8,128)(2,1)} async-done(((bf16[256,4096]{1,0:T(8,128)(2,1)}), bf16[1024,4096]{1,0:T(8,128)(2,1)}) %all-gather.12.cloned.1.call-update) | async-done | bytes 8388624 | tf_op jit(solution)/shard_map/all_gather | solution.py:96
  651.4 12.1 %convolution_convert_fusion.1 = bf16[896,4096]{1,0:T(8,128)(2,1)} fusion(bf16[1024,896]{1,0:T(8,128)(2,1)S(1)} %bitcast.37, bf16[1024,4096]{1,0:T(8,128)(2,1)} %all-gather.12.cloned.1.call-done), kind=kOutput, calls=%fused_computation.1 | convolution fusion | flops 7519862784 | bytes 17563648 | tf_op jit(solution)/shard_map/dot_general | solution.py:98
  (71 shorter events, 24.4 us)
Async XLA Ops:
  7.2 52.6 %all-gather.6.cloned.1.call-start = ((), (), s32[]{:S(2)}) async-start(), calls=%async_computation.4 | async-start | bytes 2064384 | tf_op jit(solution)/shard_map/all_gather | solution.py:34
  9.8 175.5 %all-reduce.2.cloned.1.call-start = ((), (), s32[]{:S(2)}) async-start(), calls=%async_computation.5 | async-start | bytes 3670016 | tf_op jit(solution)/shard_map/psum | solution.py:40
  75.0 15.5 %copy-start = (bf16[256,4096]{1,0:T(8,128)(2,1)}, bf16[256,4096]{1,0:T(8,128)(2,1)S(1)}, u32[]{:S(2)}) copy-start(bf16[256,4096]{1,0:T(8,128)(2,1)S(1)} %get-tuple-element.4) | copy-start | bytes 6291460
  75.0 15.8 %copy-start.5 = (bf16[3584]{0:T(1024)(128)(2,1)S(1)}, bf16[3584]{0:T(1024)(128)(2,1)}, u32[]{:S(2)}) copy-start(bf16[3584]{0:T(1024)(128)(2,1)} %param.16) | copy-start | bytes 21508
  75.0 15.8 %copy-start.6 = (bf16[3584]{0:T(1024)(128)(2,1)S(1)}, bf16[3584]{0:T(1024)(128)(2,1)}, u32[]{:S(2)}) copy-start(bf16[3584]{0:T(1024)(128)(2,1)} %param.17) | copy-start | bytes 21508
  90.5 177.2 %reduce-scatter.7.cloned.1.call-start = ((), (), s32[]{:S(2)}) async-start(), calls=%async_computation.10 | async-start | bytes 2064384
  185.2 9.6 %slice-start = ((s8[6422528]{0:T(1024)(128)(4,1)}), s8[4194304]{0:T(1024)(128)(4,1)S(1)}, s32[]{:S(2)}) async-start(s8[6422528]{0:T(1024)(128)(4,1)} %bitcast.29), calls=%async_computation.12 | async-start | bytes 8388608
  189.2 5.7 slice-start.1
  189.2 5.7 copy-start.3
  189.2 7.9 %slice-start.4 = ((s8[6422528]{0:T(1024)(128)(4,1)}), s8[4194304]{0:T(1024)(128)(4,1)S(1)}, s32[]{:S(2)}) async-start(s8[6422528]{0:T(1024)(128)(4,1)} %bitcast.41), calls=%async_computation.16 | async-start | bytes 8388608
  194.9 2.2 slice-start.5
  197.1 4.4 copy-start.4
  201.4 154.0 %all-gather.8.cloned.1.call-start = ((), (), s32[]{:S(2)}) async-start(), calls=%async_computation.6 | async-start | bytes 2064384 | tf_op jit(solution)/shard_map/all_gather | solution.py:66
  309.2 126.3 %reduce-scatter.9.cloned.1.call-start = ((), (), s32[]{:S(2)}) async-start(), calls=%async_computation.11 | async-start | bytes 2064384
  355.3 11.1 %slice-start.2 = ((s8[6422528]{0:T(1024)(128)(4,1)}), s8[2228224]{0:T(1024)(128)(4,1)S(1)}, s32[]{:S(2)}) async-start(s8[6422528]{0:T(1024)(128)(4,1)} %bitcast.31), calls=%async_computation.14 | async-start | bytes 4456448
  361.0 5.5 slice-start.3
  370.1 134.3 %all-gather.10.cloned.1.call-start = ((), (), s32[]{:S(2)}) async-start(), calls=%async_computation.7 | async-start | bytes 2064384 | tf_op jit(solution)/shard_map/all_gather | solution.py:85
  459.7 143.3 %all-gather.14.cloned.1.call-start = ((), (), s32[]{:S(2)}) async-start(), calls=%async_computation.9 | async-start | bytes 10485760 | tf_op jit(solution)/shard_map/all_gather | solution.py:95
  460.4 191.0 %all-gather.12.cloned.1.call-start = ((), (), s32[]{:S(2)}) async-start(), calls=%async_computation.8 | async-start | bytes 10485760 | tf_op jit(solution)/shard_map/all_gather | solution.py:96
  504.5 18.4 %copy-start.1 = (bf16[256,3584]{0,1:T(8,128)(2,1)S(1)}, bf16[256,3584]{0,1:T(8,128)(2,1)}, u32[]{:S(2)}) copy-start(bf16[256,3584]{0,1:T(8,128)(2,1)} %all-gather.6.cloned.1.call-done) | copy-start | bytes 5505028
  569.0 31.6 %all-to-all-start.1 = ((bf16[256,4,896]{0,2,1:T(8,128)(2,1)}), bf16[256,4,896]{0,2,1:T(8,128)(2,1)S(1)}, u32[]{:S(2)}, u32[]{:S(2)}) async-start(bf16[256,4,896]{0,2,1:T(8,128)(2,1)} %bitcast.36), calls=%async_computation.1 | async-start | bytes 3670016 | tf_op jit(solution)/shard_map/all_to_all | solution.py:92
  603.0 48.5 %copy-start.2 = (bf16[4,256,896]{2,1,0:T(8,128)(2,1)S(1)}, bf16[4,256,896]{2,1,0:T(8,128)(2,1)}, u32[]{:S(2)}) copy-start(bf16[4,256,896]{2,1,0:T(8,128)(2,1)} %copy.34) | copy-start | bytes 5505028
Sparse Core Ops, SparseCore 0:
  10.6 49.1 all-gather.5
  90.6 94.5 all-reduce.1
  201.5 66.1 reduce-scatter.6
  309.4 45.9 all-gather.7
  370.3 65.1 reduce-scatter.8
  459.8 44.6 all-gather.9
  506.0 81.8 all-gather.13
  590.1 61.2 all-gather.11
where the time goes:
time: 671 us; the launch traced here: 670 us
  waiting for transfers between devices  422 us (63%)
  matrix products  103 us (15%)
  blocking collectives  102 us (15%)
  between operations  14.4 us (2%)
  other arithmetic  13.9 us (2%)
  local copies, waits for them, and re-layouts  10.9 us (2%)
    unnamed x10, waiting for transfers between devices  131 us
    psum x1, waiting for transfers between devices, per_device(): lax.psum(partial_recon.astype(jnp.bfloat16), ('tensor', 'latent'))  94.5 us
    all_gather x1, waiting for transfers between devices, per_device(): lax.all_gather(centered_share, ('tensor', 'latent'), axis=1, tiled=True)  49.3 us
    all_to_all x1, blocking collectives, per_device(): lax.all_to_all(centered, 'batch', split_axis=1, concat_axis=0, tiled=True)  46.2 us
    all_gather x1, waiting for transfers between devices, per_device(): lax.all_gather(grad_share, ('tensor', 'latent'), axis=1, tiled=True)  45.8 us
    all_gather x1, waiting for transfers between devices, per_device(): lax.all_gather(recon_share, ('tensor', 'latent'), axis=1, tiled=True)  44 us
    all_gather x1, waiting for transfers between devices, per_device(): lax.all_gather(grad_preact, 'batch', axis=0, tiled=True)  33.3 us
    all_to_all x1, waiting for transfers between devices, per_device(): lax.all_to_all(grad_recon, 'batch', split_axis=1, concat_axis=0, tiled=True)  24.1 us
  transfers between devices with their start and end apart: 9, of which 8 were waited for; matrix products, arithmetic and copies ran while one was open for 6% of the time, Pallas kernels for 0%

commit v1 on v0

--- a/solution.py
+++ b/solution.py
@@ -37,9 +37,9 @@
     )
     latents = jnp.maximum(preact, 0.0).astype(bf16)
     partial_recon = jnp.dot(latents, decoder_weight, preferred_element_type=f32)
-    recon_full = lax.psum(partial_recon.astype(jnp.bfloat16), ("tensor", "latent")).astype(
-        jnp.float32
-    ) + decoder_bias.astype(f32)
+    recon_full = jnp.sum(
+        lax.all_gather(partial_recon.astype(jnp.bfloat16), ("tensor", "latent")), axis=0
+    ).astype(jnp.float32) + decoder_bias.astype(f32)
     scale_in = lax.rsqrt(
         jnp.sum(recon_full * recon_full, axis=1, keepdims=True) / model_width + epsilon
     )

time: 671 us -> 791 us (1.18)
  waiting for transfers between devices: 422 us -> 567 us
  blocking collectives: 102 us -> 56.2 us
  other arithmetic: 13.9 us -> 24.3 us
    all_gather x0 -> x1, waiting for transfers between devices: none -> 200 us  [per_device(): lax.all_gather(partial_recon.astype(jnp.bfloat16), ('tensor', 'latent'))]
    unnamed x10 -> x8, waiting for transfers between devices: 131 us -> 0.81 us
    reduce_scatter x0 -> x2, waiting for transfers between devices: none -> 129 us  [the longest x1 65.3 us: per_device(): lax.psum_scatter(partial_input.astype(jnp.bfloat16), ('tensor', 'latent')...]
    psum x1 -> x0, waiting for transfers between devices: 94.5 us -> none  [per_device(): lax.psum(partial_recon.astype(jnp.bfloat16), ('tensor', 'latent'))]
    all_to_all x1 -> x0, blocking collectives: 46.2 us -> none  [per_device(): lax.all_to_all(centered, 'batch', split_axis=1, concat_axis=0, tiled=True)]
    all_to_all x0 -> x1, waiting for transfers between devices: none -> 39.3 us  [per_device(): lax.all_to_all(centered, 'batch', split_axis=1, concat_axis=0, tiled=True)]
    all_gather x1, waiting for transfers between devices: 0.01 us -> 10.5 us  [per_device(): lax.all_gather(latents, 'batch', axis=0, tiled=True)]
    all_to_all x1, waiting for transfers between devices: 24.1 us -> 13.9 us  [per_device(): lax.all_to_all(grad_recon, 'batch', split_axis=1, concat_axis=0, tiled=True)]
  transfers between devices with their start and end apart: 9 -> 10, of which waited for: 8 -> 10; matrix products, arithmetic and copies ran while one was open for 6% -> 5% of each run, Pallas kernels for 0% -> 0%
where the time goes in v1:
time: 791 us; the launch traced here: 785 us
  waiting for transfers between devices  567 us (72%)
  matrix products  104 us (13%)
  blocking collectives  56.2 us (7%)
  other arithmetic  24.3 us (3%)
  between operations  14.6 us (2%)
  local copies, waits for them, and re-layouts  9.18 us (1%)
  starting transfers between devices  9.01 us (1%)
    all_gather x1, waiting for transfers between devices, per_device(): lax.all_gather(partial_recon.astype(jnp.bfloat16), ('tensor', 'latent'))  200 us
    reduce_scatter x1, waiting for transfers between devices, per_device(): lax.psum_scatter(partial_input.astype(jnp.bfloat16), ('tensor', 'latent')...  65.3 us
    reduce_scatter x1, waiting for transfers between devices, per_device(): lax.psum_scatter(partial_out.astype(jnp.bfloat16), ('tensor', 'latent'),...  63.7 us
    all_gather x1, waiting for transfers between devices, per_device(): lax.all_gather(centered_share, ('tensor', 'latent'), axis=1, tiled=True)  49.3 us
    all_gather x1, waiting for transfers between devices, per_device(): lax.all_gather(grad_share, ('tensor', 'latent'), axis=1, tiled=True)  46.1 us
    all_gather x1, waiting for transfers between devices, per_device(): lax.all_gather(recon_share, ('tensor', 'latent'), axis=1, tiled=True)  43.9 us
    all_to_all x1, waiting for transfers between devices, per_device(): lax.all_to_all(centered, 'batch', split_axis=1, concat_axis=0, tiled=True)  39.3 us
    all_gather x1, waiting for transfers between devices, per_device(): lax.all_gather(grad_preact, 'batch', axis=0, tiled=True)  34.4 us
  transfers between devices with their start and end apart: 10, of which 10 were waited for; matrix products, arithmetic and copies ran while one was open for 5% of the time, Pallas kernels for 0%

profile of v1, /device:TPU:0, one launch (start us, length us, event | category | flops | bytes accessed | tf_op | source)
XLA Modules:
  0.0 785.0 jit_solution(7738846007459882668)
XLA Ops:
  10.5 49.3 %all-gather.8.cloned.1.call-done = bf16[256,3584]{0,1:T(8,128)(2,1)} async-done(((bf16[256,448]{0,1:T(8,128)(2,1)}), bf16[256,3584]{0,1:T(8,128)(2,1)}) %all-gather.8.cloned.1.call-update) | async-done | bytes 1835024 | tf_op jit(solution)/shard_map/all_gather | solution.py:34
  59.8 15.2 %maximum_convert_fusion = (bf16[256,4096]{1,0:T(8,128)(2,1)S(1)}, f32[256,4096]{1,0:T(8,128)}) fusion(f32[4096]{0:T(1024)S(1)} %convert_element_type.76, bf16[256,3584]{0,1:T(8,128)(2,1)} %all-gather.8.cloned.1.call-done, bf16[3584,4096]{1,0:T(8,128)(2,1)} %param.13), kind=kOutput, calls=%fused_computation.9 | convolution fusion | flops 7519338496 | bytes 37502976 | tf_op jit(solution)/shard_map/dot_general | solution.py:35
  75.0 15.5 %convolution_convert_fusion.2 = bf16[256,3584]{1,0:T(8,128)(2,1)} fusion(bf16[256,4096]{1,0:T(8,128)(2,1)S(1)} %get-tuple-element.4, bf16[4096,3584]{1,0:T(8,128)(2,1)} %param.15), kind=kOutput, calls=%fused_computation.5 | convolution fusion | flops 7517110272 | bytes 33292288 | tf_op jit(solution)/shard_map/dot_general | solution.py:39
  91.1 200.0 %all-gather.18.cloned.1.call-done = bf16[2048,3584]{1,0:T(8,128)(2,1)} async-done(((bf16[256,3584]{1,0:T(8,128)(2,1)}), bf16[2048,3584]{1,0:T(8,128)(2,1)}) %all-gather.18.cloned.1.call-update) | async-done | bytes 14680080 | tf_op jit(solution)/shard_map/all_gather | solution.py:41
  291.0 8.3 %reduce_sum.48 = bf16[256,3584]{1,0:T(8,128)(2,1)S(1)} reduce(bf16[8,256,3584]{2,1,0:T(8,128)(2,1)} %bitcast.25, bf16[]{:T(256)} %constant.38.clone.1), dimensions={0}, to_apply=%region_0.0 | reduce | flops 6422528 | bytes 16515074 | tf_op jit(solution)/shard_map/reduce_sum | solution.py:40
  305.8 6.5 fusion.42
  315.3 4.3 convolution_convert_fusion.3
  321.2 63.7 %reduce-scatter.3.cloned.1.call-done = bf16[256,448]{0,1:T(8,128)(2,1)} async-done(((bf16[256,3584]{0,1:T(8,128)(2,1)}), bf16[256,448]{0,1:T(8,128)(2,1)}) %reduce-scatter.3.cloned.1.call-update) | async-done | bytes 229392 | tf_op jit(solution)/shard_map/reduce_scatter | solution.py:53
  385.9 19.4 %psum.21 = f32[256]{0:T(256)S(1)} all-reduce(f32[256]{0:T(256)S(1)} %fusion.18), channel_id=1, replica_groups=mesh['batch'=4,'tensor'=2,'latent'=4] {'tensor','latent'}, use_global_device_ids=true, to_apply=%region_4.0 | all-reduce | flops 256 | bytes 2048 | tf_op jit(solution)/shard_map/psum | solution.py:56
  406.7 17.4 %psum.22 = f32[256]{0:T(256)S(1)} all-reduce(f32[256]{0:T(256)S(1)} %fusion.14), channel_id=1, replica_groups=mesh['batch'=4,'tensor'=2,'latent'=4] {'tensor','latent'}, use_global_device_ids=true, to_apply=%region_6.0 | all-reduce | flops 256 | bytes 2048 | tf_op jit(solution)/shard_map/psum | solution.py:63
  426.2 46.1 %all-gather.10.cloned.1.call-done = bf16[256,3584]{0,1:T(8,128)(2,1)} async-done(((bf16[256,448]{0,1:T(8,128)(2,1)}), bf16[256,3584]{0,1:T(8,128)(2,1)}) %all-gather.10.cloned.1.call-update) | async-done | bytes 1835024 | tf_op jit(solution)/shard_map/all_gather | solution.py:66
  472.3 5.6 fusion.43
  478.0 5.5 fusion.19
  487.3 65.3 %reduce-scatter.5.cloned.1.call-done = bf16[256,448]{0,1:T(8,128)(2,1)} async-done(((bf16[256,3584]{0,1:T(8,128)(2,1)}), bf16[256,448]{0,1:T(8,128)(2,1)}) %reduce-scatter.5.cloned.1.call-update) | async-done | bytes 229392 | tf_op jit(solution)/shard_map/reduce_scatter | solution.py:78
  553.8 19.4 %psum.23 = f32[256]{0:T(256)S(1)} all-reduce(f32[256]{0:T(256)S(1)} %multiply_reduce_fusion.1), channel_id=1, replica_groups=mesh['batch'=4,'tensor'=2,'latent'=4] {'tensor','latent'}, use_global_device_ids=true, to_apply=%region_9.0 | all-reduce | flops 256 | bytes 2048 | tf_op jit(solution)/shard_map/psum | solution.py:83
  576.2 43.9 %all-gather.12.cloned.1.call-done = bf16[256,3584]{0,1:T(8,128)(2,1)} async-done(((bf16[256,448]{0,1:T(8,128)(2,1)}), bf16[256,3584]{0,1:T(8,128)(2,1)}) %all-gather.12.cloned.1.call-update) | async-done | bytes 1835024 | tf_op jit(solution)/shard_map/all_gather | solution.py:85
  620.1 18.2 %fusion = bf16[256,4096]{1,0:T(8,128)(2,1)} fusion(bf16[256,3584]{0,1:T(8,128)(2,1)} %all-gather.12.cloned.1.call-done, bf16[4096,3584]{1,0:T(8,128)(2,1)} %param.15, f32[256,4096]{1,0:T(8,128)} %get-tuple-element.5), kind=kOutput, calls=%fused_computation.6 | convolution fusion | flops 7519338496 | bytes 37486592 | tf_op jit(solution)/shard_map/dot_general | solution.py:86
  645.4 39.3 %all-to-all-done = bf16[256,4,896]{0,2,1:T(8,128)(2,1)S(1)} async-done(((bf16[256,4,896]{0,2,1:T(8,128)(2,1)}), bf16[256,4,896]{0,2,1:T(8,128)(2,1)S(1)}, u32[]{:S(2)}, u32[]{:S(2)}) %all-to-all-start) | async-done | bytes 1835040 | tf_op jit(solution)/shard_map/all_to_all | solution.py:91
  684.8 4.6 all-to-all-start.1
  691.8 10.5 %all-gather.16.cloned.1.call-done = bf16[1024,4096]{1,0:T(8,128)(2,1)} async-done(((bf16[256,4096]{1,0:T(8,128)(2,1)}), bf16[1024,4096]{1,0:T(8,128)(2,1)}) %all-gather.16.cloned.1.call-update) | async-done | bytes 8388624 | tf_op jit(solution)/shard_map/all_gather | solution.py:95
  702.3 13.9 %all-to-all-done.1 = bf16[256,4,896]{2,0,1:T(8,128)(2,1)} async-done(((bf16[256,4,896]{2,0,1:T(8,128)(2,1)}), bf16[256,4,896]{2,0,1:T(8,128)(2,1)}, u32[]{:S(2)}, u32[]{:S(2)}) %all-to-all-start.1) | async-done | bytes 1835040 | tf_op jit(solution)/shard_map/all_to_all | solution.py:92
  716.3 15.1 %convolution_convert_fusion = bf16[4096,896]{1,0:T(8,128)(2,1)} fusion(bf16[1024,4096]{1,0:T(8,128)(2,1)} %all-gather.16.cloned.1.call-done, bf16[1024,896]{1,0:T(8,128)(2,1)} %bitcast.6), kind=kOutput, calls=%fused_computation | convolution fusion | flops 7519862784 | bytes 17563648 | tf_op jit(solution)/shard_map/dot_general | solution.py:101
  731.4 34.4 %all-gather.14.cloned.1.call-done = bf16[1024,4096]{1,0:T(8,128)(2,1)} async-done(((bf16[256,4096]{1,0:T(8,128)(2,1)}), bf16[1024,4096]{1,0:T(8,128)(2,1)}) %all-gather.14.cloned.1.call-update) | async-done | bytes 8388624 | tf_op jit(solution)/shard_map/all_gather | solution.py:96
  765.8 12.1 %convolution_convert_fusion.1 = bf16[896,4096]{1,0:T(8,128)(2,1)} fusion(bf16[1024,896]{1,0:T(8,128)(2,1)S(1)} %bitcast.33, bf16[1024,4096]{1,0:T(8,128)(2,1)} %all-gather.14.cloned.1.call-done), kind=kOutput, calls=%fused_computation.1 | convolution fusion | flops 7519862784 | bytes 17563648 | tf_op jit(solution)/shard_map/dot_general | solution.py:98
  (69 shorter events, 36.9 us)
Async XLA Ops:
  7.2 52.6 %all-gather.8.cloned.1.call-start = ((), (), s32[]{:S(2)}) async-start(), calls=%async_computation.4 | async-start | bytes 2064384 | tf_op jit(solution)/shard_map/all_gather | solution.py:34
  9.8 281.3 %all-gather.18.cloned.1.call-start = ((), (), s32[]{:S(2)}) async-start(), calls=%async_computation.11 | async-start | bytes 16515072 | tf_op jit(solution)/shard_map/all_gather | solution.py:41
  75.0 15.5 %copy-start = (bf16[256,4096]{1,0:T(8,128)(2,1)}, bf16[256,4096]{1,0:T(8,128)(2,1)S(1)}, u32[]{:S(2)}) copy-start(bf16[256,4096]{1,0:T(8,128)(2,1)S(1)} %get-tuple-element.4) | copy-start | bytes 6291460
  75.0 16.0 %copy-start.5 = (bf16[3584]{0:T(1024)(128)(2,1)S(1)}, bf16[3584]{0:T(1024)(128)(2,1)}, u32[]{:S(2)}) copy-start(bf16[3584]{0:T(1024)(128)(2,1)} %param.16) | copy-start | bytes 21508
  75.0 16.1 %copy-start.6 = (bf16[3584]{0:T(1024)(128)(2,1)S(1)}, bf16[3584]{0:T(1024)(128)(2,1)}, u32[]{:S(2)}) copy-start(bf16[3584]{0:T(1024)(128)(2,1)} %param.17) | copy-start | bytes 21508
  90.5 294.4 %reduce-scatter.3.cloned.1.call-start = ((), (), s32[]{:S(2)}) async-start(), calls=%async_computation.5 | async-start | bytes 2064384 | tf_op jit(solution)/shard_map/reduce_scatter | solution.py:53
  301.7 10.7 %slice-start = ((s8[6422528]{0:T(1024)(128)(4,1)}), s8[4194304]{0:T(1024)(128)(4,1)S(1)}, s32[]{:S(2)}) async-start(s8[6422528]{0:T(1024)(128)(4,1)} %bitcast.26), calls=%async_computation.12 | async-start | bytes 8388608
  305.8 6.5 slice-start.1
  305.8 6.5 copy-start.1
  305.8 9.5 %slice-start.4 = ((s8[6422528]{0:T(1024)(128)(4,1)}), s8[4194304]{0:T(1024)(128)(4,1)S(1)}, s32[]{:S(2)}) async-start(s8[6422528]{0:T(1024)(128)(4,1)} %bitcast.34), calls=%async_computation.16 | async-start | bytes 8388608
  312.4 2.9 slice-start.5
  315.3 90.0 %copy-start.3 = (bf16[256,448]{0,1:T(8,128)(2,1)S(1)}, bf16[256,448]{0,1:T(8,128)(2,1)}, u32[]{:S(2)}) copy-start(bf16[256,448]{0,1:T(8,128)(2,1)} %param.12) | copy-start | bytes 688132
  319.6 152.7 %all-gather.10.cloned.1.call-start = ((), (), s32[]{:S(2)}) async-start(), calls=%async_computation.6 | async-start | bytes 2064384 | tf_op jit(solution)/shard_map/all_gather | solution.py:66
  426.1 126.4 %reduce-scatter.5.cloned.1.call-start = ((), (), s32[]{:S(2)}) async-start(), calls=%async_computation.7 | async-start | bytes 2064384 | tf_op jit(solution)/shard_map/reduce_scatter | solution.py:78
  472.3 11.1 %slice-start.2 = ((s8[6422528]{0:T(1024)(128)(4,1)}), s8[2228224]{0:T(1024)(128)(4,1)S(1)}, s32[]{:S(2)}) async-start(s8[6422528]{0:T(1024)(128)(4,1)} %bitcast.28), calls=%async_computation.14 | async-start | bytes 4456448
  478.0 5.5 slice-start.3
  483.5 89.8 %copy-start.2 = (bf16[256,448]{0,1:T(8,128)(2,1)S(1)}, bf16[256,448]{0,1:T(8,128)(2,1)}, u32[]{:S(2)}) copy-start(bf16[256,448]{0,1:T(8,128)(2,1)} %reduce-scatter.3.cloned.1.call-done) | copy-start | bytes 688132
  487.1 132.9 %all-gather.12.cloned.1.call-start = ((), (), s32[]{:S(2)}) async-start(), calls=%async_computation.8 | async-start | bytes 2064384 | tf_op jit(solution)/shard_map/all_gather | solution.py:85
  575.4 127.0 %all-gather.16.cloned.1.call-start = ((), (), s32[]{:S(2)}) async-start(), calls=%async_computation.10 | async-start | bytes 10485760 | tf_op jit(solution)/shard_map/all_gather | solution.py:95
  576.1 189.7 %all-gather.14.cloned.1.call-start = ((), (), s32[]{:S(2)}) async-start(), calls=%async_computation.9 | async-start | bytes 10485760 | tf_op jit(solution)/shard_map/all_gather | solution.py:96
  638.2 46.5 %all-to-all-start = ((bf16[256,4,896]{0,2,1:T(8,128)(2,1)}), bf16[256,4,896]{0,2,1:T(8,128)(2,1)S(1)}, u32[]{:S(2)}, u32[]{:S(2)}) async-start(bf16[256,4,896]{0,2,1:T(8,128)(2,1)} %bitcast.31), calls=%async_computation | async-start | bytes 3670016 | tf_op jit(solution)/shard_map/all_to_all | solution.py:91
  684.8 31.5 %all-to-all-start.1 = ((bf16[256,4,896]{2,0,1:T(8,128)(2,1)}), bf16[256,4,896]{2,0,1:T(8,128)(2,1)}, u32[]{:S(2)}, u32[]{:S(2)}) async-start(bf16[256,4,896]{2,0,1:T(8,128)(2,1)} %copy.18), calls=%async_computation.3 | async-start | bytes 3670016 | tf_op jit(solution)/shard_map/all_to_all | solution.py:92
  716.3 49.6 %copy-start.4 = (bf16[4,256,896]{2,1,0:T(8,128)(2,1)S(1)}, bf16[4,256,896]{2,1,0:T(8,128)(2,1)}, u32[]{:S(2)}) copy-start(bf16[4,256,896]{2,1,0:T(8,128)(2,1)} %copy.16) | copy-start | bytes 5505028
Sparse Core Ops, SparseCore 0:
  10.6 49.1 all-gather.7
  90.6 200.3 all-gather.17
  319.8 65.0 reduce-scatter.2
  426.3 46.0 all-gather.9
  487.3 65.2 reduce-scatter.4
  575.5 44.5 all-gather.11
  621.6 80.6 all-gather.15
  704.5 61.3 all-gather.13
